TPU v7x, 32 devices: a whole 2x2x4 slice. The times are simulated.
32 devices in a mesh: wide: 8 (over y, x, core), narrow: 4 (over z).
Axes of the slice: x: 2, y: 2, z: 4, core: 2. Of those that a mesh axis runs over, the one named last changes fastest.
Arguments:
- tokens: bfloat16 [8192, 2048], P(('wide', 'narrow')), may hold values from -6 to 6
- out_grad: bfloat16 [8192, 2048], P(('wide', 'narrow')), may hold values from -6 to 6
- captions: bfloat16 [4096, 4096], P(('wide', 'narrow')), may hold values from -6 to 6
- image_blocks: int32 [32, 256], P('wide'), may hold values from 0 to 3, never falling along the last dimension, each value on 1 to 128 neighbouring positions
- caption_owner: int32 [8, 512], P('wide'), may hold values from 0 to 3, never falling along the last dimension, each value on 1 to 256 neighbouring positions
- norm_gains: float32 [3, 2048], replicated, may hold values from 0.25 to 1.75
- norm_shifts: float32 [3, 2048], replicated, may hold values from -3 to 3
- w_query: float32 [2048, 2048], P('wide', 'narrow'), may hold values from -0.125 to 0.125
- w_key: float32 [2048, 2048], P('wide', 'narrow'), may hold values from -0.125 to 0.125
- w_value: float32 [2048, 2048], P('wide', 'narrow'), may hold values from -0.125 to 0.125
- w_out: float32 [2048, 2048], P('narrow', 'wide'), may hold values from -0.375 to 0.375
- w_cross_query: float32 [2048, 2048], P('wide', 'narrow'), may hold values from -0.125 to 0.125
- w_cross_key: float32 [4096, 2048], P('wide', 'narrow'), may hold values from -0.09375 to 0.09375
- w_cross_value: float32 [4096, 2048], P('wide', 'narrow'), may hold values from -0.09375 to 0.09375
- w_cross_out: float32 [2048, 2048], P('narrow', 'wide'), may hold values from -0.375 to 0.375
- w_up: float32 [2048, 8192], P('wide', 'narrow'), may hold values from -0.125 to 0.125
- w_down: float32 [8192, 2048], P('narrow', 'wide'), may hold values from -0.0625 to 0.0625
Outputs:
- block_out: bfloat16 [8192, 2048], P(('wide', 'narrow'))
- grad_tokens: bfloat16 [8192, 2048], P(('wide', 'narrow'))
- grad_captions: bfloat16 [4096, 4096], P(('wide', 'narrow'))
- grad_norm_gains: float32 [3, 2048], replicated
- grad_norm_shifts: float32 [3, 2048], replicated
- grad_w_query: float32 [2048, 2048], P('wide', 'narrow')
- grad_w_key: float32 [2048, 2048], P('wide', 'narrow')
- grad_w_value: float32 [2048, 2048], P('wide', 'narrow')
- grad_w_out: float32 [2048, 2048], P('narrow', 'wide')
- grad_w_cross_query: float32 [2048, 2048], P('wide', 'narrow')
- grad_w_cross_key: float32 [4096, 2048], P('wide', 'narrow')
- grad_w_cross_value: float32 [4096, 2048], P('wide', 'narrow')
- grad_w_cross_out: float32 [2048, 2048], P('narrow', 'wide')
- grad_w_up: float32 [2048, 8192], P('wide', 'narrow')
- grad_w_down: float32 [8192, 2048], P('narrow', 'wide')
Inputs may be any that keep to these rules, and one draw needn't show every extreme that they name: `image_blocks`: within an image the block numbers never fall; each of the 4 blocks has 1 to 128 tokens, and one block of every image has exactly that many. `caption_owner`: within a group the owners never fall; every image of the group has 1 to 256 caption tokens, and one image of every group has exactly 256.
All inputs are finite; a program needn't handle non-finite values.
Results may differ from a plain program's by a relative error of at most 0.024.
Values may be sent and summed in bfloat16 or wider, within the bound.
A program may use at most 320 MiB of HBM per device.

v0:
```python
import jax
import jax.numpy as jnp
from jax import lax
from jax.sharding import PartitionSpec as P

HEAD_DIM = 128
PIX = 256
CHUNKS = 2
EPSILON = 1e-06
MASKED = -1000000000.0
BF = jnp.bfloat16
F32 = jnp.float32


def product(left_side, right_side):
    return lax.dot_general(
        left_side, right_side, (((left_side.ndim - 1,), (0,)), ((), ())), preferred_element_type=F32
    )


def right_inner(left_side, right_side):
    return lax.dot_general(
        left_side, right_side, (((left_side.ndim - 1,), (1,)), ((), ())), preferred_element_type=F32
    )


def left_inner(left_side, right_side):
    rows = tuple(range(left_side.ndim - 1))
    return lax.dot_general(
        left_side, right_side, ((rows, rows), ((), ())), preferred_element_type=F32
    )


def spread(rows):
    n = lax.axis_size("narrow")
    here = lax.axis_index("narrow")
    up, down = ([rows], [rows])
    for step in range(1, n):
        up.append(lax.ppermute(up[-1], "narrow", [(k, k + 1) for k in range(step - 1, n - 1)]))
        down.append(lax.ppermute(down[-1], "narrow", [(k, k - 1) for k in range(1, n - step + 1)]))
    parts = [rows] + [jnp.where(here >= s, up[s], down[n - s]) for s in range(1, n)]
    return jnp.stack(parts)


def sink(parts):
    n = lax.axis_size("narrow")
    up = down = None
    for step in range(1, n):
        one, other = (parts[step], parts[n - step])
        if up is not None:
            one = up.astype(F32) + one.astype(F32)
            other = down.astype(F32) + other.astype(F32)
        up = lax.ppermute(one.astype(BF), "narrow", [(k, k + 1) for k in range(step)])
        down = lax.ppermute(other.astype(BF), "narrow", [(k, k - 1) for k in range(n - step, n)])
    return up.astype(F32) + down.astype(F32) + parts[0].astype(F32)


def norm_stats(features):
    center = features - jnp.mean(features, axis=-1, keepdims=True)
    rstd = lax.rsqrt(jnp.mean(center * center, axis=-1, keepdims=True) + EPSILON)
    return (center * rstd, rstd)


def norm_back(grad, xhat, rstd, gain):
    scaled = grad * gain
    return rstd * (
        scaled
        - jnp.mean(scaled, axis=-1, keepdims=True)
        - xhat * jnp.mean(scaled * xhat, axis=-1, keepdims=True)
    )


def norm_sums(grad, xhat):
    return jnp.stack([jnp.sum(grad * xhat, axis=0), jnp.sum(grad, axis=0)])


def score_block(queries, keys_in, allowed, score_scale):
    raw = jnp.einsum("iphe,iqhe->ihpq", queries, keys_in, preferred_element_type=F32)
    return jnp.where(allowed[:, None], raw * score_scale, MASKED)


def attend(queries, keys_in, values_in, allowed, score_scale):
    scores = score_block(queries, keys_in, allowed, score_scale)
    log_total = jax.nn.logsumexp(scores, axis=-1, keepdims=True)
    soft = jnp.exp(scores - log_total).astype(BF)
    mixture = jnp.einsum("ihpq,iqhe->iphe", soft, values_in, preferred_element_type=F32)
    return (mixture.astype(BF), log_total)


def attend_back(queries, keys_in, values_in, allowed, log_total, grad_mix, score_scale):
    soft = jnp.exp(score_block(queries, keys_in, allowed, score_scale) - log_total)
    grad_soft = jnp.einsum("iphe,iqhe->ihpq", grad_mix, values_in, preferred_element_type=F32)
    grad_values = jnp.einsum(
        "ihpq,iphe->iqhe", soft.astype(BF), grad_mix, preferred_element_type=F32
    )
    row_dot = jnp.sum(soft * grad_soft, axis=-1, keepdims=True)
    grad_scores = (soft * (grad_soft - row_dot) * score_scale).astype(BF)
    grad_queries = jnp.einsum("ihpq,iqhe->iphe", grad_scores, keys_in, preferred_element_type=F32)
    grad_keys = jnp.einsum("ihpq,iphe->iqhe", grad_scores, queries, preferred_element_type=F32)
    return (grad_queries.astype(BF), grad_keys, grad_values)


def after(value, *others):
    return lax.optimization_barrier((value, *others))[0]


def follow(value, other):
    return value + (other[(0,) * other.ndim].astype(F32) * 0.0).astype(value.dtype)


def exchange_sum(value):
    for axis in ("wide", "narrow"):
        size = lax.axis_size(axis)
        step = 1
        while step < size:
            value = value + lax.ppermute(value, axis, [(k, k ^ step) for k in range(size)])
            step *= 2
    return value


def body(
    tokens,
    out_grad,
    captions,
    image_blocks,
    caption_owner,
    norm_gains,
    norm_shifts,
    w_query,
    w_key,
    w_value,
    w_out,
    w_cross_query,
    w_cross_key,
    w_cross_value,
    w_cross_out,
    w_up,
    w_down,
):
    scale = HEAD_DIM ** (-0.5)
    n = lax.axis_size("narrow")
    here = lax.axis_index("narrow")
    width = w_query.shape[1]
    heads = width // HEAD_DIM
    part = PIX // CHUNKS
    chunks = [slice(c * part, (c + 1) * part) for c in range(CHUNKS)]
    image_of = (here - jnp.arange(n)) % n

    def relative(blocks):
        return jnp.stack(
            [lax.dynamic_index_in_dim(blocks, image_of[s], 0, False) for s in range(n)]
        )

    def rows_of(*pieces):
        return lax.all_gather(
            jnp.concatenate([p.astype(BF) for p in pieces], axis=1), "wide", axis=0, tiled=True
        )

    def columns_of(piece):
        return lax.all_gather(piece.astype(BF), "wide", axis=1, tiled=True)

    def to_rows(g):
        return lax.psum_scatter(g.astype(BF), "wide", scatter_dimension=0, tiled=True).astype(F32)

    def to_columns(g):
        return lax.psum_scatter(g.astype(BF), "wide", scatter_dimension=1, tiled=True).astype(F32)

    full_qkv = rows_of(w_query, w_key, w_value)
    full_out = columns_of(w_out)
    full_ckv = rows_of(w_cross_key, w_cross_value)
    full_cq = rows_of(w_cross_query)
    full_cout = columns_of(w_cross_out)
    full_up = rows_of(w_up)
    full_down = columns_of(w_down)
    residual0 = tokens.astype(F32)
    xhat1, rstd1 = norm_stats(residual0)
    own1 = (xhat1 * norm_gains[0] + norm_shifts[0]).astype(BF)
    normed1 = spread(own1)
    qkv = product(normed1, full_qkv).astype(BF)
    heads_of = lambda x: x.reshape(x.shape[:-1] + (x.shape[-1] // HEAD_DIM, HEAD_DIM))
    self_q, self_k, self_v = [heads_of(qkv[..., k * width : (k + 1) * width]) for k in range(3)]
    blocks = image_blocks[image_of]
    self_allowed = blocks[:, :, None] == blocks[:, None, :]
    self_mix, self_total = attend(self_q, self_k, self_v, self_allowed, scale)
    self_mix = self_mix.reshape(n, PIX, width)
    text_rows = lax.all_gather(captions, "narrow", axis=0, tiled=True)
    text_count, text_width = text_rows.shape
    ckv = product(text_rows, full_ckv).astype(BF)
    cross_k = heads_of(ckv[None, :, :width])
    cross_v = heads_of(ckv[None, :, width:])
    owner = caption_owner[0]
    part_image = jnp.repeat(image_of, part)
    cross_allowed = (part_image[:, None] == owner[None, :])[None]
    state = []
    for rows in chunks:
        residual1 = residual0[rows] + sink(product(self_mix[:, rows], full_out).astype(BF))
        xhat2, rstd2 = norm_stats(residual1)
        state.append((residual1, xhat2, rstd2))
    normed2 = [spread((s[1] * norm_gains[1] + norm_shifts[1]).astype(BF)) for s in state]
    grad_all = relative(lax.all_gather(out_grad, "narrow", axis=0))
    cross_q, cross_mix, cross_total, state3 = ([], [], [], [])
    for c in range(CHUNKS):
        q = heads_of(product(normed2[c], full_cq).astype(BF).reshape(1, n * part, width))
        mix, total = attend(q, cross_k, cross_v, cross_allowed, scale)
        mix = mix.reshape(n, part, width)
        residual2 = state[c][0] + sink(product(mix, full_cout).astype(BF))
        xhat3, rstd3 = norm_stats(residual2)
        cross_q.append(q)
        cross_mix.append(mix)
        cross_total.append(total)
        state3.append((residual2, xhat3, rstd3))
    normed3 = [spread((s[1] * norm_gains[2] + norm_shifts[2]).astype(BF)) for s in state3]
    out_parts, acts, grad_hiddens, grad2, sums3 = ([], [], [], [], [])
    for c, rows in enumerate(chunks):
        if c > 0:
            normed3[c] = follow(normed3[c], sent)
        hidden = product(normed3[c], full_up)
        grad_rows = grad_all[:, rows]
        acted, gelu_back = jax.vjp(jax.nn.gelu, hidden)
        acted = acted.astype(BF)
        grad_hidden = gelu_back(right_inner(grad_rows, full_down))[0].astype(BF)
        acts.append(acted)
        grad_hiddens.append(grad_hidden)
        sent = lax.optimization_barrier(right_inner(grad_hidden, full_up).astype(BF))
        grad_n3 = sink(sent)
        residual2, xhat3, rstd3 = state3[c]
        sums3.append(norm_sums(grad_n3, xhat3))
        grad2.append(out_grad[rows].astype(F32) + norm_back(grad_n3, xhat3, rstd3, norm_gains[2]))
        out_parts.append(product(acted, full_down).astype(BF))
    cat = lambda xs: jnp.concatenate(xs, axis=1)
    acted, grad_hidden, n3 = (cat(acts), cat(grad_hiddens), cat(normed3))
    grad_down = left_inner(acted, cat([grad_all[:, rows] for rows in chunks]))
    grad_up = left_inner(n3, grad_hidden)
    out_sum = lax.psum_scatter(relative(cat(out_parts)), "narrow", scatter_dimension=0)
    block_out = (jnp.concatenate([s[0] for s in state3]) + out_sum.astype(F32)).astype(BF)
    e2 = [spread(g.astype(BF)) for g in grad2]
    own_down = to_columns(grad_down)
    own_up = to_rows(grad_up)
    e2[-1] = after(e2[-1], grad_down, grad_up)
    grad1, sums2, grad_cqs, grad_ck, grad_cv = ([], [], [], 0.0, 0.0)
    for c in range(CHUNKS):
        grad_mix = heads_of(right_inner(e2[c], full_cout).astype(BF).reshape(1, n * part, width))
        gq, gk, gv = attend_back(
            cross_q[c], cross_k, cross_v, cross_allowed, cross_total[c], grad_mix, scale
        )
        gq = gq.reshape(n, part, width)
        grad_cqs.append(gq)
        grad_ck = grad_ck + gk
        grad_cv = grad_cv + gv
        grad_n2 = sink(right_inner(gq, full_cq).astype(BF))
        _, xhat2, rstd2 = state[c]
        sums2.append(norm_sums(grad_n2, xhat2))
        grad1.append(grad2[c] + norm_back(grad_n2, xhat2, rstd2, norm_gains[1]))
    grad_cout = left_inner(cat(cross_mix), cat(e2))
    grad_cq = left_inner(cat(normed2), cat(grad_cqs))
    grad_ckv = jnp.concatenate(
        [grad_ck.reshape(text_count, width), grad_cv.reshape(text_count, width)], axis=1
    ).astype(BF)
    grad_text_part = right_inner(grad_ckv, full_ckv).astype(BF).reshape(n, -1, text_width)
    grad_wckv = left_inner(text_rows, grad_ckv)
    e1 = [spread(g.astype(BF)) for g in grad1]
    own_cout = to_columns(grad_cout)
    own_cq = to_rows(grad_cq)
    own_ckv = to_rows(grad_wckv)
    e1[-1] = after(e1[-1], grad_cout, grad_cq, grad_wckv, grad_text_part)
    grad_mix = heads_of(cat([right_inner(e, full_out).astype(BF) for e in e1]))
    grad_mix = after(grad_mix, own_down, own_up)
    gq, gk, gv = attend_back(self_q, self_k, self_v, self_allowed, self_total, grad_mix, scale)
    grad_qkv = jnp.concatenate([g.astype(BF).reshape(n, PIX, width) for g in (gq, gk, gv)], axis=-1)
    grad_out = left_inner(self_mix, cat(e1))
    grad_wqkv = left_inner(normed1, grad_qkv)
    grad_n1 = sink(right_inner(after(grad_qkv, grad_wqkv), full_qkv).astype(BF))
    grad_text = sink(relative(after(grad_text_part, grad_mix))).astype(BF)
    grad1 = jnp.concatenate(grad1)
    grad_n1 = after(grad_n1, own_cout, own_cq, own_ckv)
    grad_tokens = (grad1 + norm_back(grad_n1, xhat1, rstd1, norm_gains[0])).astype(BF)
    sums = exchange_sum(jnp.stack([norm_sums(grad_n1, xhat1), sum(sums2), sum(sums3)]))
    own_out = to_columns(grad_out)
    own_qkv = to_rows(grad_wqkv)
    return (
        block_out,
        grad_tokens,
        grad_text,
        sums[:, 0],
        sums[:, 1],
        own_qkv[:, :width],
        own_qkv[:, width : 2 * width],
        own_qkv[:, 2 * width :],
        own_out,
        own_cq,
        own_ckv[:, :width],
        own_ckv[:, width:],
        own_cout,
        own_up,
        own_down,
    )


def solution(mesh):
    in_specs = (
        P(("wide", "narrow"), None),
        P(("wide", "narrow"), None),
        P(("wide", "narrow"), None),
        P("wide", None),
        P("wide", None),
        P(),
        P(),
        P("wide", "narrow"),
        P("wide", "narrow"),
        P("wide", "narrow"),
        P("narrow", "wide"),
        P("wide", "narrow"),
        P("wide", "narrow"),
        P("wide", "narrow"),
        P("narrow", "wide"),
        P("wide", "narrow"),
        P("narrow", "wide"),
    )
    out_specs = (
        P(("wide", "narrow"), None),
        P(("wide", "narrow"), None),
        P(("wide", "narrow"), None),
        P(),
        P(),
        P("wide", "narrow"),
        P("wide", "narrow"),
        P("wide", "narrow"),
        P("narrow", "wide"),
        P("wide", "narrow"),
        P("wide", "narrow"),
        P("wide", "narrow"),
        P("narrow", "wide"),
        P("wide", "narrow"),
        P("narrow", "wide"),
    )
    return jax.shard_map(body, mesh=mesh, in_specs=in_specs, out_specs=out_specs, check_vma=False)
```

profile of v0, /device:TPU:0, one launch (start us, length us, event | category | flops | bytes accessed | tf_op | source)
XLA Modules:
  0.0 1377.7 jit_solution(2369147938922174307)
XLA Ops:
  28.0 21.0 %collective-permute-done = bf16[256,2048]{1,0:T(8,128)(2,1)S(1)} collective-permute-done((bf16[256,2048]{1,0:T(8,128)(2,1)S(1)}, bf16[256,2048]{1,0:T(8,128)(2,1)S(1)}, u32[]{:S(2)}, u32[]{:S(2)}) %collective-permute-start) | collective-permute-done | bytes 1048608 | tf_op jit(solution)/shard_map/ppermute | solution.py:39
  57.5 22.6 %collective-permute-done.2 = bf16[256,2048]{1,0:T(8,128)(2,1)} collective-permute-done((bf16[256,2048]{1,0:T(8,128)(2,1)S(1)}, bf16[256,2048]{1,0:T(8,128)(2,1)}, u32[]{:S(2)}, u32[]{:S(2)}) %collective-permute-start.2) | collective-permute-done | bytes 1048608 | tf_op jit(solution)/shard_map/ppermute | solution.py:40
  85.7 19.9 %collective-permute-done.3 = bf16[256,2048]{1,0:T(8,128)(2,1)S(1)} collective-permute-done((bf16[256,2048]{1,0:T(8,128)(2,1)}, bf16[256,2048]{1,0:T(8,128)(2,1)S(1)}, u32[]{:S(2)}, u32[]{:S(2)}) %collective-permute-start.3) | collective-permute-done | bytes 1048608 | tf_op jit(solution)/shard_map/ppermute | solution.py:40
  133.5 18.8 %collective-permute-done.6 = bf16[128,2048]{1,0:T(8,128)(2,1)S(1)} collective-permute-done((bf16[128,2048]{1,0:T(8,128)(2,1)S(1)}, bf16[128,2048]{1,0:T(8,128)(2,1)S(1)}, u32[]{:S(2)}, u32[]{:S(2)}) %collective-permute-start.6) | collective-permute-done | bytes 524320 | tf_op jit(solution)/shard_map/ppermute | solution.py:53
  157.7 17.1 %collective-permute-done.24 = bf16[128,2048]{1,0:T(8,128)(2,1)S(1)} collective-permute-done((bf16[128,2048]{1,0:T(8,128)(2,1)S(1)}, bf16[128,2048]{1,0:T(8,128)(2,1)S(1)}, u32[]{:S(2)}, u32[]{:S(2)}) %collective-permute-start.24) | collective-permute-done | bytes 524320 | tf_op jit(solution)/shard_map/ppermute | solution.py:53
  180.2 17.0 %collective-permute-done.7 = bf16[128,2048]{1,0:T(8,128)(2,1)S(1)} collective-permute-done((bf16[128,2048]{1,0:T(8,128)(2,1)S(1)}, bf16[128,2048]{1,0:T(8,128)(2,1)S(1)}, u32[]{:S(2)}, u32[]{:S(2)}) %collective-permute-start.7) | collective-permute-done | bytes 524320 | tf_op jit(solution)/shard_map/ppermute | solution.py:53
  203.4 16.4 %collective-permute-done.25 = bf16[128,2048]{1,0:T(8,128)(2,1)S(1)} collective-permute-done((bf16[128,2048]{1,0:T(8,128)(2,1)S(1)}, bf16[128,2048]{1,0:T(8,128)(2,1)S(1)}, u32[]{:S(2)}, u32[]{:S(2)}) %collective-permute-start.25) | collective-permute-done | bytes 524320 | tf_op jit(solution)/shard_map/ppermute | solution.py:53
  226.3 15.9 %collective-permute-done.8 = bf16[128,2048]{1,0:T(8,128)(2,1)S(1)} collective-permute-done((bf16[128,2048]{1,0:T(8,128)(2,1)S(1)}, bf16[128,2048]{1,0:T(8,128)(2,1)S(1)}, u32[]{:S(2)}, u32[]{:S(2)}) %collective-permute-start.8) | collective-permute-done | bytes 524320 | tf_op jit(solution)/shard_map/ppermute | solution.py:53
  242.2 19.3 %collective-permute-done.26 = bf16[128,2048]{1,0:T(8,128)(2,1)S(1)} collective-permute-done((bf16[128,2048]{1,0:T(8,128)(2,1)S(1)}, bf16[128,2048]{1,0:T(8,128)(2,1)S(1)}, u32[]{:S(2)}, u32[]{:S(2)}) %collective-permute-start.26) | collective-permute-done | bytes 524320 | tf_op jit(solution)/shard_map/ppermute | solution.py:53
  373.6 19.3 %collective-permute-done.18 = bf16[128,2048]{1,0:T(8,128)(2,1)S(1)} collective-permute-done((bf16[128,2048]{1,0:T(8,128)(2,1)S(1)}, bf16[128,2048]{1,0:T(8,128)(2,1)S(1)}, u32[]{:S(2)}, u32[]{:S(2)}) %collective-permute-start.18) | collective-permute-done | bytes 524320 | tf_op jit(solution)/shard_map/ppermute | solution.py:53
  398.4 17.0 %collective-permute-done.36 = bf16[128,2048]{1,0:T(8,128)(2,1)S(1)} collective-permute-done((bf16[128,2048]{1,0:T(8,128)(2,1)S(1)}, bf16[128,2048]{1,0:T(8,128)(2,1)S(1)}, u32[]{:S(2)}, u32[]{:S(2)}) %collective-permute-start.36) | collective-permute-done | bytes 524320 | tf_op jit(solution)/shard_map/ppermute | solution.py:53
  420.8 17.0 %collective-permute-done.19 = bf16[128,2048]{1,0:T(8,128)(2,1)S(1)} collective-permute-done((bf16[128,2048]{1,0:T(8,128)(2,1)S(1)}, bf16[128,2048]{1,0:T(8,128)(2,1)S(1)}, u32[]{:S(2)}, u32[]{:S(2)}) %collective-permute-start.19) | collective-permute-done | bytes 524320 | tf_op jit(solution)/shard_map/ppermute | solution.py:53
  444.0 16.4 %collective-permute-done.37 = bf16[128,2048]{1,0:T(8,128)(2,1)S(1)} collective-permute-done((bf16[128,2048]{1,0:T(8,128)(2,1)S(1)}, bf16[128,2048]{1,0:T(8,128)(2,1)S(1)}, u32[]{:S(2)}, u32[]{:S(2)}) %collective-permute-start.37) | collective-permute-done | bytes 524320 | tf_op jit(solution)/shard_map/ppermute | solution.py:53
  466.4 15.7 %collective-permute-done.20 = bf16[128,2048]{1,0:T(8,128)(2,1)S(1)} collective-permute-done((bf16[128,2048]{1,0:T(8,128)(2,1)S(1)}, bf16[128,2048]{1,0:T(8,128)(2,1)S(1)}, u32[]{:S(2)}, u32[]{:S(2)}) %collective-permute-start.20) | collective-permute-done | bytes 524320 | tf_op jit(solution)/shard_map/ppermute | solution.py:53
  482.8 14.0 %collective-permute-done.38 = bf16[128,2048]{1,0:T(8,128)(2,1)S(1)} collective-permute-done((bf16[128,2048]{1,0:T(8,128)(2,1)S(1)}, bf16[128,2048]{1,0:T(8,128)(2,1)S(1)}, u32[]{:S(2)}, u32[]{:S(2)}) %collective-permute-start.38) | collective-permute-done | bytes 524320 | tf_op jit(solution)/shard_map/ppermute | solution.py:53
  563.9 11.9 multiply_convert_fusion.4
  575.8 32.7 %all-gather.25.cloned.1.call-done = bf16[2048,2048]{1,0:T(8,128)(2,1)} async-done(((bf16[2048,256]{1,0:T(8,128)(2,1)}), bf16[2048,2048]{1,0:T(8,128)(2,1)}) %all-gather.25.cloned.1.call-update) | async-done | bytes 8388624 | tf_op jit(solution)/shard_map/all_gather | solution.py:160
  646.2 13.5 convolution_bitcast_fusion.2
  659.7 14.4 %convolution_bitcast_fusion.3 = bf16[2048,2048]{1,0:T(8,128)(2,1)} fusion(bf16[4,128,2048]{2,1,0:T(8,128)(2,1)} %get-tuple-element.189, bf16[4,128,2048]{2,1,0:T(8,128)(2,1)} %get-tuple-element.187, bf16[1,256,2048]{2,1,0:T(8,128)(2,1)} %copy-done.45, bf16[1,256,2048]{2,1,0:T(8,128)(2,1)} %copy-done.46, bf16[1,256,2048]{2,1,0:T(8,128)(2,1)} %copy-done.47, ...), kind=kOutput, calls=%fused_computation.7 | convolution fusion | flops 8604614656 | bytes 16777216 | tf_op jit(solution)/shard_map/dot_general | solution.py:29
  736.0 10.8 collective-permute-done.74
  804.9 18.6 %collective-permute-done.81 = bf16[128,2048]{1,0:T(8,128)(2,1)S(1)} collective-permute-done((bf16[128,2048]{1,0:T(8,128)(2,1)S(1)}, bf16[128,2048]{1,0:T(8,128)(2,1)S(1)}, u32[]{:S(2)}, u32[]{:S(2)}) %collective-permute-start.81) | collective-permute-done | bytes 524320 | tf_op jit(solution)/shard_map/ppermute | solution.py:40
  932.9 10.6 collective-permute-start.85
  947.9 20.0 %collective-permute-start.68 = (bf16[128,2048]{1,0:T(8,128)(2,1)}, bf16[128,2048]{1,0:T(8,128)(2,1)}, u32[]{:S(2)}, u32[]{:S(2)}) collective-permute-start(bf16[128,2048]{1,0:T(8,128)(2,1)} %get-tuple-element.99), channel_id=1, source_target_pairs={{0,1},{1,2},{2,3},{4,5},{5,6},{6,7},{8,9},{9,10},{10,11},{12,13},{... | collective-permute-start | bytes 1572872 | tf_op jit(solution)/shard_map/ppermute | solution.py:53
  981.3 11.5 collective-permute-start.86
  996.2 16.9 %collective-permute-done.86 = bf16[128,2048]{1,0:T(8,128)(2,1)S(1)} collective-permute-done((bf16[128,2048]{1,0:T(8,128)(2,1)S(1)}, bf16[128,2048]{1,0:T(8,128)(2,1)S(1)}, u32[]{:S(2)}, u32[]{:S(2)}) %collective-permute-start.86) | collective-permute-done | bytes 524320 | tf_op jit(solution)/shard_map/ppermute | solution.py:53
  1019.9 25.2 %collective-permute-start.96 = (bf16[128,2048]{1,0:T(8,128)(2,1)S(1)}, bf16[128,2048]{1,0:T(8,128)(2,1)S(1)}, u32[]{:S(2)}, u32[]{:S(2)}) collective-permute-start(bf16[128,2048]{1,0:T(8,128)(2,1)S(1)} %get-tuple-element.68), channel_id=1, source_target_pairs={{0,1},{1,2},{2,3},{4,5},{5,6},{6,7},{8,9},{9,10},{10,11},{12,13},{... | collective-permute-start | bytes 1572872 | tf_op jit(solution)/shard_map/ppermute | solution.py:39
  1088.5 11.1 collective-permute-done.99
  1189.1 17.9 %collective-permute-done.102 = bf16[256,2048]{1,0:T(8,128)(2,1)S(1)} collective-permute-done((bf16[256,2048]{1,0:T(8,128)(2,1)S(1)}, bf16[256,2048]{1,0:T(8,128)(2,1)S(1)}, u32[]{:S(2)}, u32[]{:S(2)}) %collective-permute-start.102) | collective-permute-done | bytes 1048608 | tf_op jit(solution)/shard_map/ppermute | solution.py:53
  1237.7 14.3 %collective-permute-done.103 = bf16[256,2048]{1,0:T(8,128)(2,1)} collective-permute-done((bf16[256,2048]{1,0:T(8,128)(2,1)}, bf16[256,2048]{1,0:T(8,128)(2,1)}, u32[]{:S(2)}, u32[]{:S(2)}) %collective-permute-start.103) | collective-permute-done | bytes 1048608 | tf_op jit(solution)/shard_map/ppermute | solution.py:53
  1284.8 12.2 collective-permute-done.104
  1321.9 19.2 %collective-permute-start.118 = (f32[3,2,2048]{2,0,1:T(4,128)S(1)}, f32[3,2,2048]{2,0,1:T(4,128)S(1)}, u32[]{:S(2)}, u32[]{:S(2)}) collective-permute-start(f32[3,2,2048]{2,0,1:T(4,128)S(1)} %add.569), channel_id=1, source_target_pairs={{0,2},{1,3},{2,0},{3,1},{4,6},{5,7},{6,4},{7,5},{8,10},{9,11},{10,... | collective-permute-start | bytes 147464 | tf_op jit(solution)/shard_map/ppermute | solution.py:116
  1344.0 20.7 %collective-permute-done.118 = f32[3,2,2048]{2,0,1:T(4,128)S(1)} collective-permute-done((f32[3,2,2048]{2,0,1:T(4,128)S(1)}, f32[3,2,2048]{2,0,1:T(4,128)S(1)}, u32[]{:S(2)}, u32[]{:S(2)}) %collective-permute-start.118) | collective-permute-done | bytes 49184 | tf_op jit(solution)/shard_map/ppermute | solution.py:116
  (774 shorter events, 803.0 us)
Async XLA Ops:
  7.2 99.4 %all-gather.11.cloned.1.call-start = ((), (), s32[]{:S(2)}) async-start(), calls=%async_computation.8 | async-start | bytes 7077888 | tf_op jit(solution)/shard_map/all_gather | solution.py:155
  11.6 112.8 %all-gather.13.cloned.1.call-start = ((), (), s32[]{:S(2)}) async-start(), calls=%async_computation.9 | async-start | bytes 2359296 | tf_op jit(solution)/shard_map/all_gather | solution.py:160
  12.4 310.2 %all-gather.19.cloned.1.call-start = ((), (), s32[]{:S(2)}) async-start(), calls=%async_computation.12 | async-start | bytes 2359296 | tf_op jit(solution)/shard_map/all_gather | solution.py:155
  13.2 325.2 %all-gather.17.cloned.1.call-start = ((), (), s32[]{:S(2)}) async-start(), calls=%async_computation.11 | async-start | bytes 5242880 | tf_op jit(solution)/shard_map/all_gather | solution.py:186
  13.8 324.6 %all-gather.15.cloned.1.call-start = ((), (), s32[]{:S(2)}) async-start(), calls=%async_computation.10 | async-start | bytes 9437184 | tf_op jit(solution)/shard_map/all_gather | solution.py:155
  16.5 346.2 %all-gather.21.cloned.1.call-start = ((), (), s32[]{:S(2)}) async-start(), calls=%async_computation.13 | async-start | bytes 2359296 | tf_op jit(solution)/shard_map/all_gather | solution.py:160
  18.4 507.8 %all-gather.27.cloned.1.call-start = ((), (), s32[]{:S(2)}) async-start(), calls=%async_computation.24 | async-start | bytes 5242880 | tf_op jit(solution)/shard_map/all_gather | solution.py:200
  19.2 544.7 %all-gather.23.cloned.1.call-start = ((), (), s32[]{:S(2)}) async-start(), calls=%async_computation.14 | async-start | bytes 9437184 | tf_op jit(solution)/shard_map/all_gather | solution.py:155
  20.4 588.1 %all-gather.25.cloned.1.call-start = ((), (), s32[]{:S(2)}) async-start(), calls=%async_computation.15 | async-start | bytes 9437184 | tf_op jit(solution)/shard_map/all_gather | solution.py:160
  131.5 43.3 %collective-permute-start.24 = (bf16[128,2048]{1,0:T(8,128)(2,1)S(1)}, bf16[128,2048]{1,0:T(8,128)(2,1)S(1)}, u32[]{:S(2)}, u32[]{:S(2)}) collective-permute-start(bf16[128,2048]{1,0:T(8,128)(2,1)S(1)} %get-tuple-element.147), channel_id=1, source_target_pairs={{0,1},{4,5},{8,9},{12,13},{16,17},{20,21},{24,25},{28,29}} | collective-permute-start | bytes 1572872 | tf_op jit(solution)/shard_map/ppermute | solution.py:53
  152.6 44.7 %collective-permute-start.7 = (bf16[128,2048]{1,0:T(8,128)(2,1)S(1)}, bf16[128,2048]{1,0:T(8,128)(2,1)S(1)}, u32[]{:S(2)}, u32[]{:S(2)}) collective-permute-start(bf16[128,2048]{1,0:T(8,128)(2,1)S(1)} %get-tuple-element.139), channel_id=1, source_target_pairs={{0,1},{1,2},{4,5},{5,6},{8,9},{9,10},{12,13},{13,14},{16,17},{17,1... | collective-permute-start | bytes 1572872 | tf_op jit(solution)/shard_map/ppermute | solution.py:53
  175.1 44.6 %collective-permute-start.25 = (bf16[128,2048]{1,0:T(8,128)(2,1)S(1)}, bf16[128,2048]{1,0:T(8,128)(2,1)S(1)}, u32[]{:S(2)}, u32[]{:S(2)}) collective-permute-start(bf16[128,2048]{1,0:T(8,128)(2,1)S(1)} %get-tuple-element.145), channel_id=1, source_target_pairs={{0,1},{1,2},{4,5},{5,6},{8,9},{9,10},{12,13},{13,14},{16,17},{17,1... | collective-permute-start | bytes 1572872 | tf_op jit(solution)/shard_map/ppermute | solution.py:53
  197.7 44.5 %collective-permute-start.8 = (bf16[128,2048]{1,0:T(8,128)(2,1)S(1)}, bf16[128,2048]{1,0:T(8,128)(2,1)S(1)}, u32[]{:S(2)}, u32[]{:S(2)}) collective-permute-start(bf16[128,2048]{1,0:T(8,128)(2,1)S(1)} %get-tuple-element.137), channel_id=1, source_target_pairs={{0,1},{1,2},{2,3},{4,5},{5,6},{6,7},{8,9},{9,10},{10,11},{12,13},{... | collective-permute-start | bytes 1572872 | tf_op jit(solution)/shard_map/ppermute | solution.py:53
  279.0 839.9 %reduce-scatter.13.cloned.1.call-start = ((), (), s32[]{:S(2)}) async-start(), calls=%async_computation.18 | async-start | bytes 9437184 | tf_op jit(solution)/shard_map/reduce_scatter | solution.py:163
  371.6 43.8 %collective-permute-start.36 = (bf16[128,2048]{1,0:T(8,128)(2,1)S(1)}, bf16[128,2048]{1,0:T(8,128)(2,1)S(1)}, u32[]{:S(2)}, u32[]{:S(2)}) collective-permute-start(bf16[128,2048]{1,0:T(8,128)(2,1)S(1)} %get-tuple-element.133), channel_id=1, source_target_pairs={{0,1},{4,5},{8,9},{12,13},{16,17},{20,21},{24,25},{28,29}} | collective-permute-start | bytes 1572872 | tf_op jit(solution)/shard_map/ppermute | solution.py:53
  393.2 44.6 %collective-permute-start.19 = (bf16[128,2048]{1,0:T(8,128)(2,1)S(1)}, bf16[128,2048]{1,0:T(8,128)(2,1)S(1)}, u32[]{:S(2)}, u32[]{:S(2)}) collective-permute-start(bf16[128,2048]{1,0:T(8,128)(2,1)S(1)} %get-tuple-element.125), channel_id=1, source_target_pairs={{0,1},{1,2},{4,5},{5,6},{8,9},{9,10},{12,13},{13,14},{16,17},{17,1... | collective-permute-start | bytes 1572872 | tf_op jit(solution)/shard_map/ppermute | solution.py:53
  415.7 44.6 %collective-permute-start.37 = (bf16[128,2048]{1,0:T(8,128)(2,1)S(1)}, bf16[128,2048]{1,0:T(8,128)(2,1)S(1)}, u32[]{:S(2)}, u32[]{:S(2)}) collective-permute-start(bf16[128,2048]{1,0:T(8,128)(2,1)S(1)} %get-tuple-element.131), channel_id=1, source_target_pairs={{0,1},{1,2},{4,5},{5,6},{8,9},{9,10},{12,13},{13,14},{16,17},{17,1... | collective-permute-start | bytes 1572872 | tf_op jit(solution)/shard_map/ppermute | solution.py:53
  438.2 43.9 %collective-permute-start.20 = (bf16[128,2048]{1,0:T(8,128)(2,1)S(1)}, bf16[128,2048]{1,0:T(8,128)(2,1)S(1)}, u32[]{:S(2)}, u32[]{:S(2)}) collective-permute-start(bf16[128,2048]{1,0:T(8,128)(2,1)S(1)} %get-tuple-element.123), channel_id=1, source_target_pairs={{0,1},{1,2},{2,3},{4,5},{5,6},{6,7},{8,9},{9,10},{10,11},{12,13},{... | collective-permute-start | bytes 1572872 | tf_op jit(solution)/shard_map/ppermute | solution.py:53
  538.9 86.1 %collective-permute-start.51 = (bf16[128,2048]{1,0:T(8,128)(2,1)}, bf16[128,2048]{1,0:T(8,128)(2,1)}, u32[]{:S(2)}, u32[]{:S(2)}) collective-permute-start(bf16[128,2048]{1,0:T(8,128)(2,1)} %collective-permute-done.50), channel_id=1, source_target_pairs={{1,0},{5,4},{9,8},{13,12},{17,16},{21,20},{25,24},{29,28}} | collective-permute-start | bytes 1572872 | tf_op jit(solution)/shard_map/ppermute | solution.py:40
  552.9 73.3 %collective-permute-start.53 = (bf16[128,2048]{1,0:T(8,128)(2,1)}, bf16[128,2048]{1,0:T(8,128)(2,1)}, u32[]{:S(2)}, u32[]{:S(2)}) collective-permute-start(bf16[128,2048]{1,0:T(8,128)(2,1)} %collective-permute-done.52), channel_id=1, source_target_pairs={{2,3},{6,7},{10,11},{14,15},{18,19},{22,23},{26,27},{30,31}} | collective-permute-start | bytes 1572872 | tf_op jit(solution)/shard_map/ppermute | solution.py:39
  659.7 462.1 %reduce-scatter.11.cloned.1.call-start = ((), (), s32[]{:S(2)}) async-start(), calls=%async_computation.17 | async-start | bytes 9437184 | tf_op jit(solution)/shard_map/reduce_scatter | solution.py:166
  674.2 541.5 %reduce-scatter.15.cloned.1.call-start = ((), (), s32[]{:S(2)}) async-start(), calls=%async_computation.19 | async-start | bytes 2359296 | tf_op jit(solution)/shard_map/reduce_scatter | solution.py:166
  829.3 388.2 %reduce-scatter.17.cloned.1.call-start = ((), (), s32[]{:S(2)}) async-start(), calls=%async_computation.20 | async-start | bytes 2359296 | tf_op jit(solution)/shard_map/reduce_scatter | solution.py:163
  872.6 389.6 %reduce-scatter.9.cloned.1.call-start = ((), (), s32[]{:S(2)}) async-start(), calls=%async_computation.16 | async-start | bytes 5242880 | tf_op jit(solution)/shard_map/reduce_scatter | solution.py:234
  893.2 371.6 %reduce-scatter.23.cloned.1.call-start = ((), (), s32[]{:S(2)}) async-start(), calls=%async_computation.23 | async-start | bytes 2359296 | tf_op jit(solution)/shard_map/reduce_scatter | solution.py:166
  932.9 46.7 %collective-permute-start.85 = (bf16[128,2048]{1,0:T(8,128)(2,1)}, bf16[128,2048]{1,0:T(8,128)(2,1)}, u32[]{:S(2)}, u32[]{:S(2)}) collective-permute-start(bf16[128,2048]{1,0:T(8,128)(2,1)} %get-tuple-element.113), channel_id=1, source_target_pairs={{0,1},{1,2},{4,5},{5,6},{8,9},{9,10},{12,13},{13,14},{16,17},{17,1... | collective-permute-start | bytes 1572872 | tf_op jit(solution)/shard_map/ppermute | solution.py:53
  947.9 46.2 %collective-permute-start.68 = (bf16[128,2048]{1,0:T(8,128)(2,1)}, bf16[128,2048]{1,0:T(8,128)(2,1)}, u32[]{:S(2)}, u32[]{:S(2)}) collective-permute-start(bf16[128,2048]{1,0:T(8,128)(2,1)} %get-tuple-element.99), channel_id=1, source_target_pairs={{0,1},{1,2},{2,3},{4,5},{5,6},{6,7},{8,9},{9,10},{10,11},{12,13},{... | collective-permute-start | bytes 1572872 | tf_op jit(solution)/shard_map/ppermute | solution.py:53
  1111.2 189.2 %reduce-scatter.19.cloned.1.call-start = ((), (), s32[]{:S(2)}) async-start(), calls=%async_computation.21 | async-start | bytes 9437184 | tf_op jit(solution)/shard_map/reduce_scatter | solution.py:163
  1111.8 256.9 %reduce-scatter.21.cloned.1.call-start = ((), (), s32[]{:S(2)}) async-start(), calls=%async_computation.22 | async-start | bytes 7077888 | tf_op jit(solution)/shard_map/reduce_scatter | solution.py:163
  1208.6 43.4 %collective-permute-start.103 = (bf16[256,2048]{1,0:T(8,128)(2,1)}, bf16[256,2048]{1,0:T(8,128)(2,1)}, u32[]{:S(2)}, u32[]{:S(2)}) collective-permute-start(bf16[256,2048]{1,0:T(8,128)(2,1)} %get-tuple-element.84), channel_id=1, source_target_pairs={{0,1},{1,2},{4,5},{5,6},{8,9},{9,10},{12,13},{13,14},{16,17},{17,1... | collective-permute-start | bytes 3145736 | tf_op jit(solution)/shard_map/ppermute | solution.py:53
  1277.7 87.7 %collective-permute-start.110 = (bf16[128,4096]{1,0:T(8,128)(2,1)}, bf16[128,4096]{1,0:T(8,128)(2,1)}, u32[]{:S(2)}, u32[]{:S(2)}) collective-permute-start(bf16[128,4096]{1,0:T(8,128)(2,1)} %get-tuple-element.64), channel_id=1, source_target_pairs={{0,1},{1,2},{2,3},{4,5},{5,6},{6,7},{8,9},{9,10},{10,11},{12,13},{... | collective-permute-start | bytes 3145736 | tf_op jit(solution)/shard_map/ppermute | solution.py:53
  1318.8 46.6 %collective-permute-start.113 = (bf16[128,4096]{1,0:T(8,128)(2,1)}, bf16[128,4096]{1,0:T(8,128)(2,1)}, u32[]{:S(2)}, u32[]{:S(2)}) collective-permute-start(bf16[128,4096]{1,0:T(8,128)(2,1)} %add_convert_fusion), channel_id=1, source_target_pairs={{1,0},{2,1},{3,2},{5,4},{6,5},{7,6},{9,8},{10,9},{11,10},{13,12},{... | collective-permute-start | bytes 3145736 | tf_op jit(solution)/shard_map/ppermute | solution.py:54
  (244 other events, 5869.8 us)
Sparse Core Ops, SparseCore 0:
  11.7 48.1 all-gather.10
  62.3 28.0 all-gather.12
  92.9 27.7 all-gather.18
  122.2 140.3 all-gather.16
  264.8 56.8 all-gather.14
  323.5 28.0 all-gather.20
  353.2 138.1 all-gather.26
  493.9 56.2 all-gather.22
  552.6 55.8 all-gather.24
  659.8 71.4 reduce-scatter.12
  734.8 71.2 reduce-scatter.10
  829.4 46.3 reduce-scatter.14
  879.1 41.1 reduce-scatter.16
  922.4 120.6 reduce-scatter.8
  1111.3 42.6 reduce-scatter.22
  1157.3 71.3 reduce-scatter.18
  1231.9 61.7 reduce-scatter.20
where the time goes:
time: 1390 us; the launch traced here: 1380 us
  waiting for transfers between devices  580 us (42%)
  starting transfers between devices  322 us (23%)
  matrix products  290 us (21%)
  other arithmetic  112 us (8%)
  local copies, waits for them, and re-layouts  48 us (3%)
  between operations  25.5 us (2%)
    ppermute x30, waiting for transfers between devices, sink(): lax.ppermute(one.astype(BF), 'narrow', [(k, k + 1) for k in range(step)])  320 us
    ppermute x27, waiting for transfers between devices, spread(): lax.ppermute(down[-1], 'narrow', [(k, k - 1) for k in range(1, n - step +...  177 us
    ppermute x30, starting transfers between devices, sink(): lax.ppermute(one.astype(BF), 'narrow', [(k, k + 1) for k in range(step)])  142 us
    ppermute x27, starting transfers between devices, spread(): lax.ppermute(up[-1], 'narrow', [(k, k + 1) for k in range(step - 1, n - 1)])  86.5 us
    dot_general x12, matrix products, product(): lax.dot_general(left_side, right_side, (((left_side.ndim - 1,), (0,)), ((...  75.1 us
    dot_general x12, matrix products, right_inner(): lax.dot_general(left_side, right_side, (((left_side.ndim - 1,), (1,)), ((...  69.7 us
    dot_general x7, matrix products, left_inner(): lax.dot_general(left_side, right_side, ((rows, rows), ((), ())), preferre...  57.3 us
    ppermute x27, starting transfers between devices, spread(): lax.ppermute(down[-1], 'narrow', [(k, k - 1) for k in range(1, n - step +...  35.1 us
  transfers between devices with their start and end apart: 136, of which 51 were waited for; matrix products, arithmetic and copies ran while one was open for 29% of the time, Pallas kernels for 0%

commit v1 on v0

--- a/solution.py
+++ b/solution.py
@@ -10,6 +10,18 @@
 MASKED = -1000000000.0
 BF = jnp.bfloat16
 F32 = jnp.float32
+
+
+def collect(shard, axis, dim):
+    ways, here, step = (lax.axis_size(axis), lax.axis_index(axis), shard.shape[dim])
+    line, have = (shard, 1)
+    while have < ways:
+        line = jnp.concatenate(
+            [line, lax.ppermute(line, axis, [(d, (d - have) % ways) for d in range(ways)])],
+            axis=dim,
+        )
+        have = 2 * have
+    return jnp.roll(line, here * step, axis=dim)
 
 
 def product(left_side, right_side):
@@ -157,7 +169,7 @@
         )
 
     def columns_of(piece):
-        return lax.all_gather(piece.astype(BF), "wide", axis=1, tiled=True)
+        return collect(piece.astype(BF), "wide", 1)
 
     def to_rows(g):
         return lax.psum_scatter(g.astype(BF), "wide", scatter_dimension=0, tiled=True).astype(F32)

time: 1390 us -> 1380 us (level)
  waiting for transfers between devices: 580 us -> 513 us
  local copies, waits for them, and re-layouts: 48 us -> 72.6 us
  other arithmetic: 112 us -> 133 us
    ppermute x30, waiting for transfers between devices: 320 us -> 220 us  [sink(): lax.ppermute(one.astype(BF), 'narrow', [(k, k + 1) for k in range(step)])]
    all_gather x1, waiting for transfers between devices: 0.02 us -> 51.5 us  [body(): grad_all = relative(lax.all_gather(out_grad, 'narrow', axis=0))]
    ppermute x0 -> x9, waiting for transfers between devices: none -> 38.2 us  [collect(): lax.ppermute(line, axis, [(d, (d - have) % ways) for d in range(ways)])]
    ppermute x27, waiting for transfers between devices: 177 us -> 139 us  [spread(): lax.ppermute(down[-1], 'narrow', [(k, k - 1) for k in range(1, n - step +...]
    all_gather x3 -> x0, waiting for transfers between devices: 32.8 us -> none  [columns_of(): return lax.all_gather(piece.astype(BF), 'wide', axis=1, tiled=True)]
    ppermute x0 -> x9, starting transfers between devices: none -> 32.2 us  [collect(): lax.ppermute(line, axis, [(d, (d - have) % ways) for d in range(ways)])]
    ppermute x30, starting transfers between devices: 142 us -> 125 us  [sink(): lax.ppermute(one.astype(BF), 'narrow', [(k, k + 1) for k in range(step)])]
  transfers between devices with their start and end apart: 136 -> 142, of which waited for: 51 -> 57; matrix products, arithmetic and copies ran while one was open for 29% -> 33% of each run, Pallas kernels for 0% -> 0%
where the time goes in v1:
time: 1380 us; the launch traced here: 1370 us
  waiting for transfers between devices  513 us (37%)
  starting transfers between devices  332 us (24%)
  matrix products  288 us (21%)
  other arithmetic  133 us (10%)
  local copies, waits for them, and re-layouts  72.6 us (5%)
  between operations  26.7 us (2%)
    ppermute x30, waiting for transfers between devices, sink(): lax.ppermute(one.astype(BF), 'narrow', [(k, k + 1) for k in range(step)])  220 us
    ppermute x27, waiting for transfers between devices, spread(): lax.ppermute(down[-1], 'narrow', [(k, k - 1) for k in range(1, n - step +...  139 us
    ppermute x30, starting transfers between devices, sink(): lax.ppermute(one.astype(BF), 'narrow', [(k, k + 1) for k in range(step)])  125 us
    ppermute x27, starting transfers between devices, spread(): lax.ppermute(up[-1], 'narrow', [(k, k + 1) for k in range(step - 1, n - 1)])  78.1 us
    dot_general x12, matrix products, product(): lax.dot_general(left_side, right_side, (((left_side.ndim - 1,), (0,)), ((...  76.4 us
    dot_general x12, matrix products, right_inner(): lax.dot_general(left_side, right_side, (((left_side.ndim - 1,), (1,)), ((...  72.1 us
    dot_general x7, matrix products, left_inner(): lax.dot_general(left_side, right_side, ((rows, rows), ((), ())), preferre...  52 us
    all_gather x1, waiting for transfers between devices, body(): grad_all = relative(lax.all_gather(out_grad, 'narrow', axis=0))  51.5 us
  transfers between devices with their start and end apart: 142, of which 57 were waited for; matrix products, arithmetic and copies ran while one was open for 33% of the time, Pallas kernels for 0%

profile of v1, /device:TPU:0, one launch (start us, length us, event | category | flops | bytes accessed | tf_op | source)
XLA Modules:
  0.0 1365.8 jit_solution(9194322029323017892)
XLA Ops:
  43.2 18.0 %collective-permute-done.7 = bf16[512,512]{1,0:T(8,128)(2,1)S(1)} collective-permute-done((bf16[512,512]{1,0:T(8,128)(2,1)}, bf16[512,512]{1,0:T(8,128)(2,1)S(1)}, u32[]{:S(2)}, u32[]{:S(2)}) %collective-permute-start.7) | collective-permute-done | bytes 524320 | tf_op jit(solution)/shard_map/ppermute | solution.py:20
  74.1 20.2 %collective-permute-done.8 = bf16[512,1024]{1,0:T(8,128)(2,1)} collective-permute-done((bf16[512,1024]{1,0:T(8,128)(2,1)}, bf16[512,1024]{1,0:T(8,128)(2,1)}, u32[]{:S(2)}, u32[]{:S(2)}) %collective-permute-start.8) | collective-permute-done | bytes 1048608 | tf_op jit(solution)/shard_map/ppermute | solution.py:20
  103.1 11.8 collective-permute-done.3
  116.0 10.5 fusion.95
  147.0 17.5 %collective-permute-done.9 = bf16[128,2048]{1,0:T(8,128)(2,1)S(1)} collective-permute-done((bf16[128,2048]{1,0:T(8,128)(2,1)S(1)}, bf16[128,2048]{1,0:T(8,128)(2,1)S(1)}, u32[]{:S(2)}, u32[]{:S(2)}) %collective-permute-start.9) | collective-permute-done | bytes 524320 | tf_op jit(solution)/shard_map/ppermute | solution.py:65
  164.5 10.8 collective-permute-start.22
  194.8 13.1 collective-permute-done.10
  211.2 19.2 %collective-permute-done.31 = bf16[128,2048]{1,0:T(8,128)(2,1)S(1)} collective-permute-done((bf16[128,2048]{1,0:T(8,128)(2,1)S(1)}, bf16[128,2048]{1,0:T(8,128)(2,1)S(1)}, u32[]{:S(2)}, u32[]{:S(2)}) %collective-permute-start.31) | collective-permute-done | bytes 524320 | tf_op jit(solution)/shard_map/ppermute | solution.py:65
  243.7 11.3 collective-permute-start.55
  256.3 16.8 %collective-permute-done.32 = bf16[128,2048]{1,0:T(8,128)(2,1)S(1)} collective-permute-done((bf16[128,2048]{1,0:T(8,128)(2,1)S(1)}, bf16[128,2048]{1,0:T(8,128)(2,1)S(1)}, u32[]{:S(2)}, u32[]{:S(2)}) %collective-permute-start.32) | collective-permute-done | bytes 524320 | tf_op jit(solution)/shard_map/ppermute | solution.py:65
  416.2 51.5 %all-gather.18.cloned.1.call-done = bf16[1024,2048]{1,0:T(8,128)(2,1)} async-done(((bf16[256,2048]{1,0:T(8,128)(2,1)}), bf16[1024,2048]{1,0:T(8,128)(2,1)}) %all-gather.18.cloned.1.call-update) | async-done | bytes 4194320 | tf_op jit(solution)/shard_map/all_gather | solution.py:212
  584.0 11.9 multiply_convert_fusion.4
  616.2 11.0 multiply_convert_fusion.3
  628.6 11.4 convolution_bitcast_fusion.3
  640.1 10.5 fusion.40
  652.0 11.5 convolution_bitcast_fusion.2
  770.7 11.8 collective-permute-done.71
  795.1 15.0 %collective-permute-done.90 = bf16[128,2048]{1,0:T(8,128)(2,1)S(1)} collective-permute-done((bf16[128,2048]{1,0:T(8,128)(2,1)S(1)}, bf16[128,2048]{1,0:T(8,128)(2,1)S(1)}, u32[]{:S(2)}, u32[]{:S(2)}) %collective-permute-start.90) | collective-permute-done | bytes 524320 | tf_op jit(solution)/shard_map/ppermute | solution.py:52
  847.2 9.9 fusion.265
  926.0 12.8 collective-permute-done.76
  949.0 10.2 fusion.236
  972.6 10.7 collective-permute-done.77
  985.3 14.7 %collective-permute-done.95 = bf16[128,2048]{1,0:T(8,128)(2,1)S(1)} collective-permute-done((bf16[128,2048]{1,0:T(8,128)(2,1)S(1)}, bf16[128,2048]{1,0:T(8,128)(2,1)S(1)}, u32[]{:S(2)}, u32[]{:S(2)}) %collective-permute-start.95) | collective-permute-done | bytes 524320 | tf_op jit(solution)/shard_map/ppermute | solution.py:65
  1005.2 22.6 %collective-permute-start.105 = (bf16[128,2048]{1,0:T(8,128)(2,1)S(1)}, bf16[128,2048]{1,0:T(8,128)(2,1)S(1)}, u32[]{:S(2)}, u32[]{:S(2)}) collective-permute-start(bf16[128,2048]{1,0:T(8,128)(2,1)S(1)} %get-tuple-element.69), channel_id=1, source_target_pairs={{0,1},{1,2},{2,3},{4,5},{5,6},{6,7},{8,9},{9,10},{10,11},{12,13},{... | collective-permute-start | bytes 1572872 | tf_op jit(solution)/shard_map/ppermute | solution.py:51
  1057.3 10.2 convolution_convert_fusion
  1160.1 10.1 fusion.98
  1177.5 18.1 %collective-permute-done.111 = bf16[256,2048]{1,0:T(8,128)(2,1)S(1)} collective-permute-done((bf16[256,2048]{1,0:T(8,128)(2,1)S(1)}, bf16[256,2048]{1,0:T(8,128)(2,1)S(1)}, u32[]{:S(2)}, u32[]{:S(2)}) %collective-permute-start.111) | collective-permute-done | bytes 1048608 | tf_op jit(solution)/shard_map/ppermute | solution.py:65
  1208.0 10.2 collective-permute-done.117
  1226.3 14.4 %collective-permute-done.112 = bf16[256,2048]{1,0:T(8,128)(2,1)} collective-permute-done((bf16[256,2048]{1,0:T(8,128)(2,1)}, bf16[256,2048]{1,0:T(8,128)(2,1)}, u32[]{:S(2)}, u32[]{:S(2)}) %collective-permute-start.112) | collective-permute-done | bytes 1048608 | tf_op jit(solution)/shard_map/ppermute | solution.py:65
  1274.4 11.3 collective-permute-done.113
  1309.7 19.2 %collective-permute-start.127 = (f32[3,2,2048]{2,0,1:T(4,128)S(1)}, f32[3,2,2048]{2,0,1:T(4,128)S(1)}, u32[]{:S(2)}, u32[]{:S(2)}) collective-permute-start(f32[3,2,2048]{2,0,1:T(4,128)S(1)} %add.588), channel_id=1, source_target_pairs={{0,2},{1,3},{2,0},{3,1},{4,6},{5,7},{6,4},{7,5},{8,10},{9,11},{10,... | collective-permute-start | bytes 147464 | tf_op jit(solution)/shard_map/ppermute | solution.py:128
  1331.8 20.7 %collective-permute-done.127 = f32[3,2,2048]{2,0,1:T(4,128)S(1)} collective-permute-done((f32[3,2,2048]{2,0,1:T(4,128)S(1)}, f32[3,2,2048]{2,0,1:T(4,128)S(1)}, u32[]{:S(2)}, u32[]{:S(2)}) %collective-permute-start.127) | collective-permute-done | bytes 49184 | tf_op jit(solution)/shard_map/ppermute | solution.py:128
  (856 shorter events, 860.2 us)
Async XLA Ops:
  7.2 108.7 %all-gather.8.cloned.1.call-start = ((), (), s32[]{:S(2)}) async-start(), calls=%async_computation.8 | async-start | bytes 7077888 | tf_op jit(solution)/shard_map/all_gather | solution.py:167
  11.6 318.9 %all-gather.14.cloned.1.call-start = ((), (), s32[]{:S(2)}) async-start(), calls=%async_computation.11 | async-start | bytes 2359296 | tf_op jit(solution)/shard_map/all_gather | solution.py:167
  13.5 332.8 %all-gather.12.cloned.1.call-start = ((), (), s32[]{:S(2)}) async-start(), calls=%async_computation.10 | async-start | bytes 5242880 | tf_op jit(solution)/shard_map/all_gather | solution.py:198
  14.2 341.9 %all-gather.10.cloned.1.call-start = ((), (), s32[]{:S(2)}) async-start(), calls=%async_computation.9 | async-start | bytes 9437184 | tf_op jit(solution)/shard_map/all_gather | solution.py:167
  15.7 452.1 %all-gather.18.cloned.1.call-start = ((), (), s32[]{:S(2)}) async-start(), calls=%async_computation.21 | async-start | bytes 5242880 | tf_op jit(solution)/shard_map/all_gather | solution.py:212
  16.3 567.7 %all-gather.16.cloned.1.call-start = ((), (), s32[]{:S(2)}) async-start(), calls=%async_computation.12 | async-start | bytes 9437184 | tf_op jit(solution)/shard_map/all_gather | solution.py:167
  18.5 45.3 %collective-permute-start = (bf16[256,2048]{1,0:T(8,128)(2,1)}, bf16[256,2048]{1,0:T(8,128)(2,1)}, u32[]{:S(2)}, u32[]{:S(2)}) collective-permute-start(bf16[256,2048]{1,0:T(8,128)(2,1)} %add_convert_fusion.4), channel_id=1, source_target_pairs={{0,1},{1,2},{2,3},{4,5},{5,6},{6,7},{8,9},{9,10},{10,11},{12,13},{... | collective-permute-start | bytes 3145736 | tf_op jit(solution)/shard_map/ppermute | solution.py:51
  24.5 46.1 %collective-permute-start.1 = (bf16[256,2048]{1,0:T(8,128)(2,1)}, bf16[256,2048]{1,0:T(8,128)(2,1)}, u32[]{:S(2)}, u32[]{:S(2)}) collective-permute-start(bf16[256,2048]{1,0:T(8,128)(2,1)} %add_convert_fusion.4), channel_id=1, source_target_pairs={{1,0},{2,1},{3,2},{5,4},{6,5},{7,6},{9,8},{10,9},{11,10},{13,12},{... | collective-permute-start | bytes 3145736 | tf_op jit(solution)/shard_map/ppermute | solution.py:52
  27.5 117.8 %collective-permute-start.21 = (bf16[512,256]{1,0:T(8,128)(2,1)S(1)}, bf16[512,256]{1,0:T(8,128)(2,1)}, u32[]{:S(2)}, u32[]{:S(2)}) collective-permute-start(bf16[512,256]{1,0:T(8,128)(2,1)S(1)} %convert_element_type.822), channel_id=1, source_target_pairs={{0,28},{4,0},{8,4},{12,8},{16,12},{20,16},{24,20},{28,24},{1,29},{... | collective-permute-start | bytes 786440 | tf_op jit(solution)/shard_map/ppermute | solution.py:20
  31.6 205.1 %collective-permute-start.54 = (bf16[2048,256]{1,0:T(8,128)(2,1)}, bf16[2048,256]{1,0:T(8,128)(2,1)S(1)}, u32[]{:S(2)}, u32[]{:S(2)}) collective-permute-start(bf16[2048,256]{1,0:T(8,128)(2,1)} %get-tuple-element.78), channel_id=1, source_target_pairs={{0,28},{4,0},{8,4},{12,8},{16,12},{20,16},{24,20},{28,24},{1,29},{... | collective-permute-start | bytes 3145736 | tf_op jit(solution)/shard_map/ppermute | solution.py:20
  32.7 1076.0 %reduce-scatter.11.cloned.1.call-start = ((), (), s32[]{:S(2)}) async-start(), calls=%async_computation.14 | async-start | bytes 9437184 | tf_op jit(solution)/shard_map/reduce_scatter | solution.py:178
  144.0 43.0 %collective-permute-start.30 = (bf16[128,2048]{1,0:T(8,128)(2,1)S(1)}, bf16[128,2048]{1,0:T(8,128)(2,1)S(1)}, u32[]{:S(2)}, u32[]{:S(2)}) collective-permute-start(bf16[128,2048]{1,0:T(8,128)(2,1)S(1)} %get-tuple-element.150), channel_id=1, source_target_pairs={{0,1},{4,5},{8,9},{12,13},{16,17},{20,21},{24,25},{28,29}} | collective-permute-start | bytes 1572872 | tf_op jit(solution)/shard_map/ppermute | solution.py:65
  207.9 77.3 %collective-permute-start.23 = (bf16[512,1024]{1,0:T(8,128)(2,1)S(1)}, bf16[512,1024]{1,0:T(8,128)(2,1)S(1)}, u32[]{:S(2)}, u32[]{:S(2)}) collective-permute-start(bf16[512,1024]{1,0:T(8,128)(2,1)S(1)} %pad_maximum_fusion.10), channel_id=1, source_target_pairs={{0,16},{4,20},{8,24},{12,28},{16,0},{20,4},{24,8},{28,12},{1,17},{... | collective-permute-start | bytes 3145736 | tf_op jit(solution)/shard_map/ppermute | solution.py:20
  243.7 49.9 %collective-permute-start.55 = (bf16[2048,512]{1,0:T(8,128)(2,1)S(1)}, bf16[2048,512]{1,0:T(8,128)(2,1)S(1)}, u32[]{:S(2)}, u32[]{:S(2)}) collective-permute-start(bf16[2048,512]{1,0:T(8,128)(2,1)S(1)} %pad_maximum_fusion.5), channel_id=1, source_target_pairs={{0,24},{4,28},{8,0},{12,4},{16,8},{20,12},{24,16},{28,20},{1,25},{... | collective-permute-start | bytes 6291464 | tf_op jit(solution)/shard_map/ppermute | solution.py:20
  297.3 226.6 %collective-permute-start.56 = (bf16[2048,1024]{1,0:T(8,128)(2,1)}, bf16[2048,1024]{1,0:T(8,128)(2,1)}, u32[]{:S(2)}, u32[]{:S(2)}) collective-permute-start(bf16[2048,1024]{1,0:T(8,128)(2,1)} %pad_maximum_fusion.1), channel_id=1, source_target_pairs={{0,16},{4,20},{8,24},{12,28},{16,0},{20,4},{24,8},{28,12},{1,17},{... | collective-permute-start | bytes 12582920 | tf_op jit(solution)/shard_map/ppermute | solution.py:20
  394.2 76.5 %collective-permute-start.24 = (bf16[128,2048]{1,0:T(8,128)(2,1)}, bf16[128,2048]{1,0:T(8,128)(2,1)S(1)}, u32[]{:S(2)}, u32[]{:S(2)}) collective-permute-start(bf16[128,2048]{1,0:T(8,128)(2,1)} %get-tuple-element.130), channel_id=1, source_target_pairs={{0,1},{4,5},{8,9},{12,13},{16,17},{20,21},{24,25},{28,29}} | collective-permute-start | bytes 1572872 | tf_op jit(solution)/shard_map/ppermute | solution.py:65
  395.5 75.2 %collective-permute-start.27 = (bf16[128,2048]{1,0:T(8,128)(2,1)}, bf16[128,2048]{1,0:T(8,128)(2,1)}, u32[]{:S(2)}, u32[]{:S(2)}) collective-permute-start(bf16[128,2048]{1,0:T(8,128)(2,1)} %get-tuple-element.131), channel_id=1, source_target_pairs={{3,2},{7,6},{11,10},{15,14},{19,18},{23,22},{27,26},{31,30}} | collective-permute-start | bytes 1572872 | tf_op jit(solution)/shard_map/ppermute | solution.py:66
  409.6 70.2 %collective-permute-start.43 = (bf16[128,2048]{1,0:T(8,128)(2,1)}, bf16[128,2048]{1,0:T(8,128)(2,1)}, u32[]{:S(2)}, u32[]{:S(2)}) collective-permute-start(bf16[128,2048]{1,0:T(8,128)(2,1)} %get-tuple-element.134), channel_id=1, source_target_pairs={{0,1},{1,2},{4,5},{5,6},{8,9},{9,10},{12,13},{13,14},{16,17},{17,1... | collective-permute-start | bytes 1572872 | tf_op jit(solution)/shard_map/ppermute | solution.py:65
  414.8 65.1 %collective-permute-start.46 = (bf16[128,2048]{1,0:T(8,128)(2,1)}, bf16[128,2048]{1,0:T(8,128)(2,1)}, u32[]{:S(2)}, u32[]{:S(2)}) collective-permute-start(bf16[128,2048]{1,0:T(8,128)(2,1)} %get-tuple-element.135), channel_id=1, source_target_pairs={{2,1},{3,2},{6,5},{7,6},{10,9},{11,10},{14,13},{15,14},{18,17},{19... | collective-permute-start | bytes 1572872 | tf_op jit(solution)/shard_map/ppermute | solution.py:66
  562.0 52.6 %collective-permute-start.62 = (bf16[128,2048]{1,0:T(8,128)(2,1)}, bf16[128,2048]{1,0:T(8,128)(2,1)}, u32[]{:S(2)}, u32[]{:S(2)}) collective-permute-start(bf16[128,2048]{1,0:T(8,128)(2,1)} %collective-permute-done.61), channel_id=1, source_target_pairs={{2,3},{6,7},{10,11},{14,15},{18,19},{22,23},{26,27},{30,31}} | collective-permute-start | bytes 1572872 | tf_op jit(solution)/shard_map/ppermute | solution.py:51
  640.0 471.5 %reduce-scatter.13.cloned.1.call-start = ((), (), s32[]{:S(2)}) async-start(), calls=%async_computation.15 | async-start | bytes 9437184 | tf_op jit(solution)/shard_map/reduce_scatter | solution.py:175
  663.5 540.8 %reduce-scatter.15.cloned.1.call-start = ((), (), s32[]{:S(2)}) async-start(), calls=%async_computation.16 | async-start | bytes 2359296 | tf_op jit(solution)/shard_map/reduce_scatter | solution.py:178
  815.6 390.6 %reduce-scatter.17.cloned.1.call-start = ((), (), s32[]{:S(2)}) async-start(), calls=%async_computation.17 | async-start | bytes 2359296 | tf_op jit(solution)/shard_map/reduce_scatter | solution.py:175
  864.6 388.7 %reduce-scatter.9.cloned.1.call-start = ((), (), s32[]{:S(2)}) async-start(), calls=%async_computation.13 | async-start | bytes 5242880 | tf_op jit(solution)/shard_map/reduce_scatter | solution.py:246
  885.0 370.8 %reduce-scatter.23.cloned.1.call-start = ((), (), s32[]{:S(2)}) async-start(), calls=%async_computation.20 | async-start | bytes 2359296 | tf_op jit(solution)/shard_map/reduce_scatter | solution.py:178
  1101.2 186.9 %reduce-scatter.19.cloned.1.call-start = ((), (), s32[]{:S(2)}) async-start(), calls=%async_computation.18 | async-start | bytes 9437184 | tf_op jit(solution)/shard_map/reduce_scatter | solution.py:175
  1101.9 254.5 %reduce-scatter.21.cloned.1.call-start = ((), (), s32[]{:S(2)}) async-start(), calls=%async_computation.19 | async-start | bytes 7077888 | tf_op jit(solution)/shard_map/reduce_scatter | solution.py:175
  1175.2 43.0 %collective-permute-start.117 = (bf16[128,4096]{1,0:T(8,128)(2,1)}, bf16[128,4096]{1,0:T(8,128)(2,1)}, u32[]{:S(2)}, u32[]{:S(2)}) collective-permute-start(bf16[128,4096]{1,0:T(8,128)(2,1)} %dynamic-slice_bitcast_fusion.1), channel_id=1, source_target_pairs={{0,1},{4,5},{8,9},{12,13},{16,17},{20,21},{24,25},{28,29}} | collective-permute-start | bytes 3145736 | tf_op jit(solution)/shard_map/ppermute | solution.py:65
  1197.3 43.4 %collective-permute-start.112 = (bf16[256,2048]{1,0:T(8,128)(2,1)}, bf16[256,2048]{1,0:T(8,128)(2,1)}, u32[]{:S(2)}, u32[]{:S(2)}) collective-permute-start(bf16[256,2048]{1,0:T(8,128)(2,1)} %get-tuple-element.87), channel_id=1, source_target_pairs={{0,1},{1,2},{4,5},{5,6},{8,9},{9,10},{12,13},{13,14},{16,17},{17,1... | collective-permute-start | bytes 3145736 | tf_op jit(solution)/shard_map/ppermute | solution.py:65
  1267.9 85.2 %collective-permute-start.119 = (bf16[128,4096]{1,0:T(8,128)(2,1)}, bf16[128,4096]{1,0:T(8,128)(2,1)}, u32[]{:S(2)}, u32[]{:S(2)}) collective-permute-start(bf16[128,4096]{1,0:T(8,128)(2,1)} %get-tuple-element.65), channel_id=1, source_target_pairs={{0,1},{1,2},{2,3},{4,5},{5,6},{6,7},{8,9},{9,10},{10,11},{12,13},{... | collective-permute-start | bytes 3145736 | tf_op jit(solution)/shard_map/ppermute | solution.py:65
  1306.6 46.6 %collective-permute-start.122 = (bf16[128,4096]{1,0:T(8,128)(2,1)}, bf16[128,4096]{1,0:T(8,128)(2,1)}, u32[]{:S(2)}, u32[]{:S(2)}) collective-permute-start(bf16[128,4096]{1,0:T(8,128)(2,1)} %add_convert_fusion), channel_id=1, source_target_pairs={{1,0},{2,1},{3,2},{5,4},{6,5},{7,6},{9,8},{10,9},{11,10},{13,12},{... | collective-permute-start | bytes 3145736 | tf_op jit(solution)/shard_map/ppermute | solution.py:66
  1309.7 42.8 %collective-permute-start.127 = (f32[3,2,2048]{2,0,1:T(4,128)S(1)}, f32[3,2,2048]{2,0,1:T(4,128)S(1)}, u32[]{:S(2)}, u32[]{:S(2)}) collective-permute-start(f32[3,2,2048]{2,0,1:T(4,128)S(1)} %add.588), channel_id=1, source_target_pairs={{0,2},{1,3},{2,0},{3,1},{4,6},{5,7},{6,4},{7,5},{8,10},{9,11},{10,... | collective-permute-start | bytes 147464 | tf_op jit(solution)/shard_map/ppermute | solution.py:128
  (279 other events, 6411.1 us)
Sparse Core Ops, SparseCore 0:
  11.7 84.6 all-gather.7
  98.9 33.0 all-gather.13
  133.6 134.1 all-gather.11
  269.5 86.6 all-gather.9
  357.6 110.1 all-gather.17
  469.5 56.6 all-gather.15
  640.1 69.4 reduce-scatter.10
  713.1 71.4 reduce-scatter.12
  815.7 38.7 reduce-scatter.14
  864.8 38.8 reduce-scatter.16
  906.0 115.7 reduce-scatter.8
  1101.3 39.2 reduce-scatter.22
  1144.1 71.2 reduce-scatter.18
  1218.6 61.7 reduce-scatter.20
